TPU v7x, 32 devices: a whole 2x2x4 slice. The times are simulated.
32 devices in a mesh: fsdp: 8 (over z, y), seq: 4 (over x, core).
Axes of the slice: x: 2, y: 2, z: 4, core: 2. Of those that a mesh axis runs over, the one named last changes fastest.
Arguments:
- tokens: bfloat16 [8, 1024, 768], P('fsdp', 'seq'), may hold values from -6 to 6
- condition: bfloat16 [8, 768], P('fsdp'), may hold values from -6 to 6
- ada_weight: bfloat16 [2, 768, 4608], P(None, 'fsdp'), may hold values from -0.21875 to 0.21875
- ada_bias: bfloat16 [2, 4608], P(None, 'fsdp'), may hold values from -3 to 3
- qkv_weight: bfloat16 [2, 768, 2304], P(None, 'fsdp'), may hold values from -0.21875 to 0.21875
- qv_bias: bfloat16 [2, 1536], P(None, 'fsdp'), may hold values from -3 to 3
- out_weight: bfloat16 [2, 768, 768], P(None, 'fsdp'), may hold values from -1.25 to 1.25
- out_bias: bfloat16 [2, 768], P(None, 'fsdp'), may hold values from -3 to 3
- up_weight: bfloat16 [2, 768, 3072], P(None, 'fsdp'), may hold values from -0.21875 to 0.21875
- up_bias: bfloat16 [2, 3072], P(None, 'fsdp'), may hold values from -3 to 3
- down_weight: bfloat16 [2, 3072, 768], P(None, 'fsdp'), may hold values from -0.109375 to 0.109375
- down_bias: bfloat16 [2, 768], P(None, 'fsdp'), may hold values from -3 to 3
- cotangent: bfloat16 [8, 1024, 768], P('fsdp', 'seq'), may hold values from -6 to 6
Outputs:
- block_out: bfloat16 [8, 1024, 768], P('fsdp', 'seq')
- grad_tokens: float32 [8, 1024, 768], P('fsdp', 'seq')
- grad_condition: float32 [8, 768], P('fsdp')
- grad_ada_weight: float32 [2, 768, 4608], P(None, 'fsdp')
- grad_ada_bias: float32 [2, 4608], P(None, 'fsdp')
- grad_qkv_weight: float32 [2, 768, 2304], P(None, 'fsdp')
- grad_qv_bias: float32 [2, 1536], P(None, 'fsdp')
- grad_out_weight: float32 [2, 768, 768], P(None, 'fsdp')
- grad_out_bias: float32 [2, 768], P(None, 'fsdp')
- grad_up_weight: float32 [2, 768, 3072], P(None, 'fsdp')
- grad_up_bias: float32 [2, 3072], P(None, 'fsdp')
- grad_down_weight: float32 [2, 3072, 768], P(None, 'fsdp')
- grad_down_bias: float32 [2, 768], P(None, 'fsdp')
All inputs are finite; a program needn't handle non-finite values.
Results may differ from a plain program's by a relative error of at most 0.017.
The roundings to bfloat16 on the way count: a program that leaves them out, or rounds other values in their place, can miss the bound.
Values may be sent and summed in bfloat16 or wider, within the bound.
A program may use at most 256 MiB of HBM per device.

v0:
```python
import jax
import jax.numpy as jnp
from jax import lax
from jax.sharding import PartitionSpec as P

HEAD_DIM = 64
SCORE_SCALE = HEAD_DIM ** (-0.5)
EPSILON = 1e-06
HIGHEST = lax.Precision.HIGHEST
F32 = jnp.float32
BF16 = jnp.bfloat16


def normalize(values):
    centred = values - jnp.mean(values, axis=-1, keepdims=True)
    inverse = lax.rsqrt(jnp.mean(centred * centred, axis=-1, keepdims=True) + EPSILON)
    return (centred * inverse, inverse)


def norm_back(gradient, normed, inverse):
    return inverse * (
        gradient
        - jnp.mean(gradient, axis=-1, keepdims=True)
        - normed * jnp.mean(gradient * normed, axis=-1, keepdims=True)
    )


def mm(a, b):
    return lax.dot_general(a, b, (((1,), (0,)), ((), ())), preferred_element_type=F32)


def mm_nt(a, b):
    return lax.dot_general(a, b, (((1,), (1,)), ((), ())), preferred_element_type=F32)


def mm_tn(a, b):
    return lax.dot_general(a, b, (((0,), (0,)), ((), ())), preferred_element_type=F32)


def split_heads(rows):
    return rows.reshape(rows.shape[0], -1, HEAD_DIM).transpose(1, 0, 2)


def join_heads(heads):
    return heads.transpose(1, 0, 2).reshape(heads.shape[1], -1)


def attend(q, k, v):
    q, k, v = (split_heads(q), split_heads(k), split_heads(v))
    scores = jnp.einsum("hqd,hkd->hqk", q, k, preferred_element_type=F32) * SCORE_SCALE
    logsum = jnp.log(jnp.sum(jnp.exp(scores), axis=-1, keepdims=True))
    prob = jnp.exp(scores - logsum).astype(BF16)
    out = jnp.einsum("hqk,hkd->hqd", prob, v, preferred_element_type=F32)
    return (join_heads(out).astype(BF16), logsum)


def attend_back(q, k, v, logsum, out_grad):
    q, k, v, out_grad = (split_heads(q), split_heads(k), split_heads(v), split_heads(out_grad))
    scores = jnp.einsum("hqd,hkd->hqk", q, k, preferred_element_type=F32) * SCORE_SCALE
    prob = jnp.exp(scores - logsum)
    dv = jnp.einsum("hqk,hqd->hkd", prob.astype(BF16), out_grad, preferred_element_type=F32)
    dp = jnp.einsum("hqd,hkd->hqk", out_grad, v, preferred_element_type=F32)
    inner = jnp.sum(prob * dp, axis=-1, keepdims=True)
    ds = (prob * (dp - inner)).astype(BF16)
    dq = jnp.einsum("hqk,hkd->hqd", ds, k, preferred_element_type=F32) * SCORE_SCALE
    dk = jnp.einsum("hqk,hqd->hkd", ds, q, preferred_element_type=F32) * SCORE_SCALE
    return [join_heads(t).astype(BF16) for t in (dq, dk, dv)]


def gelu_parts(u):
    c = 0.7978845608028654
    inner = c * (u + 0.044715 * (u * u * u))
    t = jnp.tanh(inner)
    value = 0.5 * u * (1.0 + t)
    slope = 0.5 * (1.0 + t) + 0.5 * u * (1.0 - t * t) * (c * (1.0 + 3.0 * 0.044715 * u * u))
    return (value, slope)


def per_device(
    tokens,
    condition,
    ada_weight,
    ada_bias,
    qkv_weight,
    qv_bias,
    out_weight,
    out_bias,
    up_weight,
    up_bias,
    down_weight,
    down_bias,
    cotangent,
):
    n = lax.axis_size("fsdp")
    ns = lax.axis_size("seq")
    f = lax.axis_index("fsdp")
    s = lax.axis_index("seq")
    layers, rows, width6 = ada_weight.shape
    width = rows * n
    ff = up_weight.shape[2]
    hc = width // ns
    fc = ff // (ns * n)

    def take(x, axis):
        return lax.dynamic_index_in_dim(x, s, axis, keepdims=False)

    def own(x, axis, size):
        return lax.dynamic_slice_in_dim(x, f * size, size, axis)

    w_qkv, w_rest = ([], [])
    for l in range(layers):
        q_part = take(qkv_weight[l].reshape(rows, 3, ns, hc), 2).reshape(rows, 3 * hc)
        u_part = take(up_weight[l].reshape(rows, n, ns, fc), 2).reshape(rows, n * fc)
        d_part = take(down_weight[l].reshape(ns, fc, width), 0)
        w_qkv.append(lax.all_gather(q_part, "fsdp", axis=0, tiled=True))
        rest = jnp.concatenate([u_part, d_part, out_weight[l]], axis=1)
        w_rest.append(lax.all_gather(rest, "fsdp", axis=0, tiled=True))
    fw = n * fc
    cond_float = condition.astype(F32)
    cond_act = jax.nn.silu(cond_float).astype(BF16)
    small = jnp.concatenate(
        [
            ada_bias.reshape(-1),
            qv_bias.reshape(-1),
            out_bias.reshape(-1),
            up_bias.reshape(-1),
            down_bias.reshape(-1),
            cond_act.reshape(-1),
        ]
    )
    small = lax.all_gather(small, "fsdp", axis=0, tiled=False)
    pos = 0

    def unpack(per_layer):
        nonlocal pos
        part = small[:, pos : pos + layers * per_layer].reshape(n, layers, per_layer)
        pos += layers * per_layer
        return part.transpose(1, 0, 2).reshape(layers, n * per_layer)

    ada_b = unpack(ada_bias.shape[1]).astype(F32)
    qv_b = unpack(qv_bias.shape[1]).astype(F32)
    out_b = unpack(out_bias.shape[1]).astype(F32)
    up_b = unpack(up_bias.shape[1]).astype(F32)
    down_b = unpack(down_bias.shape[1]).astype(F32)
    cond_all = small[:, pos:]
    cond_rows = own(cond_all, 1, rows)
    q_b = take(qv_b[:, :width].reshape(layers, ns, hc), 1)
    v_b = take(qv_b[:, width:].reshape(layers, ns, hc), 1)
    qkv_b = jnp.concatenate([q_b, jnp.zeros_like(q_b), v_b], axis=1)
    up_bs = take(up_b.reshape(layers, n, ns, fc), 2).reshape(layers, fw)
    mod_partial = jnp.stack([mm(cond_rows, ada_weight[l]) for l in range(layers)], axis=1)
    mod = lax.psum_scatter(mod_partial, "fsdp", scatter_dimension=0, tiled=True)[0] + ada_b
    hidden = tokens[0].astype(F32)
    saved = []
    for l in range(layers):
        shift_a, scale_a, gate_a, shift_m, scale_m, gate_m = jnp.split(mod[l], 6)
        n_a, r_a = normalize(hidden)
        attn_in = (n_a * (1.0 + scale_a) + shift_a).astype(BF16)
        attn_all = lax.all_gather(attn_in, "seq", axis=0, tiled=True)
        qkv = (mm(attn_all, w_qkv[l]) + qkv_b[l]).astype(BF16)
        q, k, v = (qkv[:, :hc], qkv[:, hc : 2 * hc], qkv[:, 2 * hc :])
        head_out, logsum = attend(q, k, v)
        tok_out = lax.all_to_all(head_out, "seq", split_axis=0, concat_axis=1, tiled=True)
        branch = mm(tok_out, w_rest[l][:, fw + width :]) + out_b[l]
        middle = hidden + gate_a * branch
        n_m, r_m = normalize(middle)
        mlp_in = (n_m * (1.0 + scale_m) + shift_m).astype(BF16)
        mlp_all = lax.all_gather(mlp_in, "seq", axis=0, tiled=True)
        up = mm(mlp_all, w_rest[l][:, :fw]) + up_bs[l]
        act = gelu_parts(up)[0].astype(BF16)
        feed = mm(act, w_rest[l][:, fw : fw + width])
        feed = lax.psum_scatter(feed, "seq", scatter_dimension=0, tiled=True) + down_b[l]
        saved.append(
            (n_a, r_a, attn_all, q, k, v, logsum, tok_out, branch, n_m, r_m, mlp_all, up, act, feed)
        )
        hidden = middle + gate_m * feed
    block_out = hidden.astype(BF16)
    g = cotangent[0].astype(F32)
    d_mods = [None] * layers
    reduced = [None] * layers
    bias_grads = [None] * layers
    for l in reversed(range(layers)):
        shift_a, scale_a, gate_a, shift_m, scale_m, gate_m = jnp.split(mod[l], 6)
        n_a, r_a, attn_all, q, k, v, logsum, tok_out, branch, n_m, r_m, mlp_all, up, act, feed = (
            saved[l]
        )
        g_feed = (gate_m * g).astype(BF16)
        d_gate_m = jnp.sum(g * feed, axis=0)
        g_feed_all = lax.all_gather(g_feed, "seq", axis=0, tiled=True)
        grad_down = mm_tn(act, g_feed_all)
        g_up = (mm_nt(g_feed_all, w_rest[l][:, fw : fw + width]) * gelu_parts(up)[1]).astype(BF16)
        grad_up = mm_tn(mlp_all, g_up)
        g_min = lax.psum_scatter(
            mm_nt(g_up, w_rest[l][:, :fw]), "seq", scatter_dimension=0, tiled=True
        )
        d_scale_m = jnp.sum(g_min * n_m, axis=0)
        d_shift_m = jnp.sum(g_min, axis=0)
        g_mid = g + norm_back(g_min * (1.0 + scale_m), n_m, r_m)
        g_branch = (gate_a * g_mid).astype(BF16)
        d_gate_a = jnp.sum(g_mid * branch, axis=0)
        grad_out = mm_tn(tok_out, g_branch)
        g_o = mm_nt(g_branch, w_rest[l][:, fw + width :]).astype(BF16)
        g_o_heads = lax.all_to_all(g_o, "seq", split_axis=1, concat_axis=0, tiled=True)
        dq, dk, dv = attend_back(q, k, v, logsum, g_o_heads)
        g_qkv = jnp.concatenate([dq, dk, dv], axis=1)
        grad_qkv = mm_tn(attn_all, g_qkv)
        g_ain = lax.psum_scatter(mm_nt(g_qkv, w_qkv[l]), "seq", scatter_dimension=0, tiled=True)
        d_scale_a = jnp.sum(g_ain * n_a, axis=0)
        d_shift_a = jnp.sum(g_ain, axis=0)
        g = g_mid + norm_back(g_ain * (1.0 + scale_a), n_a, r_a)
        d_mods[l] = jnp.concatenate(
            [d_shift_a, d_scale_a, d_gate_a, d_shift_m, d_scale_m, d_gate_m]
        )
        packed = jnp.concatenate([grad_up, grad_down, grad_out, grad_qkv], axis=1).astype(BF16)
        reduced[l] = lax.psum_scatter(packed, "fsdp", scatter_dimension=0, tiled=True)

        def place(x, axis):
            zeros = jnp.zeros(x.shape[:axis] + (ns,) + x.shape[axis + 1 :], F32)
            return lax.dynamic_update_slice_in_dim(zeros, x, s, axis)

        qv_g = place(
            jnp.stack([jnp.sum(dq.astype(F32), axis=0), jnp.sum(dv.astype(F32), axis=0)])[
                :, None, :
            ],
            1,
        )
        up_g = place(jnp.sum(g_up.astype(F32), axis=0).reshape(n, 1, fc), 1)
        bias_grads[l] = jnp.concatenate(
            [
                qv_g.reshape(n, -1),
                jnp.sum(g_branch.astype(F32), axis=0).reshape(n, -1),
                up_g.reshape(n, -1),
                jnp.sum(g_feed.astype(F32), axis=0).reshape(n, -1),
            ],
            axis=1,
        )
    red = jnp.stack(reduced)
    shared = jnp.concatenate([red[:, :, : fw + width], red[:, :, fw + 2 * width :]], axis=2)
    shared = lax.all_gather(shared, "seq", axis=0, tiled=False).astype(F32)
    grad_up = (
        shared[..., :fw]
        .reshape(ns, layers, rows, n, fc)
        .transpose(1, 2, 3, 0, 4)
        .reshape(layers, rows, ff)
    )
    grad_down = shared[..., fw : fw + width].transpose(1, 0, 2, 3).reshape(layers, ns * fc, width)
    grad_qkv = shared[..., fw + width :].reshape(ns, layers, rows, 3, hc).transpose(1, 2, 3, 0, 4)
    grad_qkv = grad_qkv.reshape(layers, rows, 3 * width)
    grad_out = lax.psum(red[:, :, fw + width : fw + 2 * width], "seq").astype(F32)
    bias = lax.psum(jnp.stack(bias_grads), ("fsdp", "seq"))
    bias = lax.dynamic_index_in_dim(bias, f, 1, keepdims=False)
    cuts = [qv_bias.shape[1], out_bias.shape[1], up_bias.shape[1], down_bias.shape[1]]
    grad_bias, at = ([], 0)
    for size in cuts:
        grad_bias.append(bias[:, at : at + size])
        at += size
    d_mod = lax.psum(jnp.stack(d_mods), "seq")
    d_mod_all = lax.all_gather(d_mod, "fsdp", axis=0, tiled=False)
    cond_rows32 = cond_rows.astype(F32)
    grad_ada = jnp.stack(
        [
            lax.dot_general(
                cond_rows32,
                d_mod_all[:, l],
                (((0,), (0,)), ((), ())),
                precision=HIGHEST,
                preferred_element_type=F32,
            )
            for l in range(layers)
        ]
    )
    grad_ada_bias = own(jnp.sum(d_mod_all, axis=0), 1, width6 // n)
    g_cond = sum(
        (
            lax.dot_general(
                d_mod_all[:, l],
                ada_weight[l].astype(F32),
                (((1,), (1,)), ((), ())),
                precision=HIGHEST,
                preferred_element_type=F32,
            )
            for l in range(layers)
        )
    )
    g_cond = lax.all_to_all(g_cond, "fsdp", split_axis=0, concat_axis=1, tiled=True)
    _, silu_back = jax.vjp(jax.nn.silu, cond_float)
    grad_condition = silu_back(g_cond)[0]
    return (
        block_out[None],
        g[None],
        grad_condition,
        grad_ada,
        grad_ada_bias,
        grad_qkv,
        grad_bias[0],
        grad_out,
        grad_bias[1],
        grad_up,
        grad_bias[2],
        grad_down,
        grad_bias[3],
    )


def solution(mesh):
    token = P("fsdp", "seq", None)
    matrix = P(None, "fsdp", None)
    vector = P(None, "fsdp")
    return jax.shard_map(
        per_device,
        mesh=mesh,
        in_specs=(token, P("fsdp", None)) + (matrix, vector) * 5 + (token,),
        out_specs=(token, token, P("fsdp", None)) + (matrix, vector) * 5,
        check_vma=False,
    )
```

profile of v0, /device:TPU:0, one launch (start us, length us, event | category | flops | bytes accessed | tf_op | source)
XLA Modules:
  0.0 1008.6 jit_solution(16156190823706369313)
XLA Ops:
  12.4 32.4 %all-gather.2 = bf16[8,1,3456]{2,1,0:T(2,128)(2,1)S(1)} all-gather(bf16[1,1,3456]{2,1,0:T(2,128)(2,1)S(1)} %reshape.391), channel_id=2, replica_groups=mesh['fsdp'=8,'seq'=4] {'fsdp'}, dimensions={0}, use_global_device_ids=true | all-gather | bytes 62208 | tf_op jit(solution)/shard_map/all_gather | solution.py:131
  50.2 71.0 %all-reduce.6.cloned.1.call-done = f32[8,2,4608]{2,1,0:T(2,128)} async-done(((f32[8,2,4608]{2,1,0:T(2,128)}), f32[8,2,4608]{2,1,0:T(2,128)}) %all-reduce.6.cloned.1.call-update) | async-done | bytes 294928
  135.6 34.4 %all_gather.51 = bf16[768,576]{1,0:T(8,128)(2,1)S(1)} all-gather(bf16[96,576]{1,0:T(8,128)(2,1)S(1)} %copy.123), channel_id=1, replica_groups=mesh['fsdp'=8,'seq'=4] {'fsdp'}, dimensions={0}, use_global_device_ids=true | all-gather | bytes 995328 | tf_op jit(solution)/shard_map/all_gather | solution.py:115
  197.6 14.9 %all-gather.15.cloned.1.call-done = bf16[768,2304]{1,0:T(8,128)(2,1)} async-done(((bf16[96,2304]{1,0:T(8,128)(2,1)}), bf16[768,2304]{1,0:T(8,128)(2,1)}) %all-gather.15.cloned.1.call-update) | async-done | bytes 3538960 | tf_op jit(solution)/shard_map/all_gather | solution.py:117
  216.7 18.2 %all-gather.17.cloned.1.call-done = bf16[1024,768]{1,0:T(8,128)(2,1)} async-done(((bf16[256,768]{1,0:T(8,128)(2,1)}), bf16[1024,768]{1,0:T(8,128)(2,1)}) %all-gather.17.cloned.1.call-update) | async-done | bytes 1572880 | tf_op jit(solution)/shard_map/all_gather | solution.py:168
  244.9 37.9 %reduce-scatter.13.cloned.1.call-done = f32[256,768]{1,0:T(8,128)} async-done(((f32[1024,768]{1,0:T(8,128)}), f32[256,768]{1,0:T(8,128)}) %reduce-scatter.13.cloned.1.call-update) | async-done | bytes 786448 | tf_op jit(solution)/shard_map/reduce_scatter | solution.py:172
  289.8 32.9 %all_gather.55 = bf16[768,576]{1,0:T(8,128)(2,1)S(1)} all-gather(bf16[96,576]{1,0:T(8,128)(2,1)S(1)} %copy.129), channel_id=1, replica_groups=mesh['fsdp'=8,'seq'=4] {'fsdp'}, dimensions={0}, use_global_device_ids=true | all-gather | bytes 995328 | tf_op jit(solution)/shard_map/all_gather | solution.py:115
  343.8 28.8 %all-gather.21.cloned.1.call-done = bf16[768,2304]{1,0:T(8,128)(2,1)} async-done(((bf16[96,2304]{1,0:T(8,128)(2,1)}), bf16[768,2304]{1,0:T(8,128)(2,1)}) %all-gather.21.cloned.1.call-update) | async-done | bytes 3538960 | tf_op jit(solution)/shard_map/all_gather | solution.py:117
  377.7 17.5 %all-gather.23.cloned.1.call-done = bf16[1024,768]{1,0:T(8,128)(2,1)} async-done(((bf16[256,768]{1,0:T(8,128)(2,1)}), bf16[1024,768]{1,0:T(8,128)(2,1)}) %all-gather.23.cloned.1.call-update) | async-done | bytes 1572880 | tf_op jit(solution)/shard_map/all_gather | solution.py:168
  400.0 17.0 %all-gather.25.cloned.1.call-done = bf16[1024,768]{1,0:T(8,128)(2,1)} async-done(((bf16[256,768]{1,0:T(8,128)(2,1)}), bf16[1024,768]{1,0:T(8,128)(2,1)}) %all-gather.25.cloned.1.call-update) | async-done | bytes 1572880 | tf_op jit(solution)/shard_map/all_gather | solution.py:189
  434.2 31.9 %reduce-scatter.17.cloned.1.call-done = f32[256,768]{1,0:T(8,128)} async-done(((f32[1024,768]{1,0:T(8,128)}), f32[256,768]{1,0:T(8,128)}) %reduce-scatter.17.cloned.1.call-update) | async-done | bytes 786448 | tf_op jit(solution)/shard_map/reduce_scatter | solution.py:193
  467.6 38.9 %reduce-scatter.15.cloned.1.call-done = f32[256,768]{1,0:T(8,128)} async-done(((f32[1024,768]{1,0:T(8,128)}), f32[256,768]{1,0:T(8,128)}) %reduce-scatter.15.cloned.1.call-update) | async-done | bytes 786448 | tf_op jit(solution)/shard_map/reduce_scatter | solution.py:172
  511.5 10.2 %all_to_all.80 = bf16[256,4,192]{0,2,1:T(8,128)(2,1)S(1)} all-to-all(bf16[256,4,192]{0,2,1:T(8,128)(2,1)S(1)} %bitcast.284), channel_id=1, replica_groups=mesh['fsdp'=8,'seq'=4] {'seq'}, dimensions={1} | all-to-all | bytes 786432 | tf_op jit(solution)/shard_map/all_to_all | solution.py:203
  553.4 38.0 %reduce-scatter.19.cloned.1.call-done = f32[256,768]{1,0:T(8,128)} async-done(((f32[1024,768]{1,0:T(8,128)}), f32[256,768]{1,0:T(8,128)}) %reduce-scatter.19.cloned.1.call-update) | async-done | bytes 786448 | tf_op jit(solution)/shard_map/reduce_scatter | solution.py:207
  595.5 19.6 %all-gather.27.cloned.1.call-done = bf16[1024,768]{1,0:T(8,128)(2,1)} async-done(((bf16[256,768]{1,0:T(8,128)(2,1)}), bf16[1024,768]{1,0:T(8,128)(2,1)}) %all-gather.27.cloned.1.call-update) | async-done | bytes 1572880 | tf_op jit(solution)/shard_map/all_gather | solution.py:189
  643.2 21.0 %reduce-scatter.21.cloned.1.call-done = f32[256,768]{1,0:T(8,128)} async-done(((f32[1024,768]{1,0:T(8,128)}), f32[256,768]{1,0:T(8,128)}) %reduce-scatter.21.cloned.1.call-update) | async-done | bytes 786448 | tf_op jit(solution)/shard_map/reduce_scatter | solution.py:193
  670.2 10.0 all_to_all.81
  680.8 11.1 %multiply_reduce_fusion = (f32[3,1024]{1,0:T(4,128)S(1)}, f32[3,1024,1024]{1,2,0:T(8,128)}) fusion(f32[3,1024,1024]{1,2,0:T(8,128)} %fusion.3, bf16[3,1024,64]{1,2,0:T(8,128)(2,1)S(1)} %bitcast.272, bf16[1024,3,64]{0,2,1:T(8,128)(2,1)S(1)} %reshape.363), kind=kOutput, calls=%fused_computation.7 | convolution fusion | flops 408941568 | bytes 25964544 | tf_op jit(solution)/shard_map/hqd,hkd->hqk/dot_general | solution.py:62
  691.9 10.3 %multiply_convert_fusion = bf16[3,1024,1024]{1,2,0:T(8,128)(2,1)S(1)} fusion(f32[3,1024,1024]{1,2,0:T(8,128)} %fusion.3, f32[3,1024,1024]{1,2,0:T(8,128)} %get-tuple-element.173, f32[3,1024]{1,0:T(4,128)S(1)} %get-tuple-element.172), kind=kLoop, calls=%fused_computation.6 | loop fusion | flops 9437184 | bytes 31469568 | tf_op jit(solution)/shard_map/convert_element_type | solution.py:64
  728.6 32.6 %reduce-scatter.27.cloned.1.call-done = bf16[96,2880]{1,0:T(8,128)(2,1)} async-done(((bf16[768,2880]{1,0:T(8,128)(2,1)}), bf16[96,2880]{1,0:T(8,128)(2,1)}) %reduce-scatter.27.cloned.1.call-update) | async-done | bytes 552976
  763.2 40.9 %psum.22 = f32[2,8,768]{2,0,1:T(2,128)S(1)} all-reduce(f32[2,8,768]{2,0,1:T(2,128)S(1)} %pad_maximum_fusion.14), channel_id=1, replica_groups=mesh['fsdp'=8,'seq'=4] {'fsdp','seq'}, use_global_device_ids=true, to_apply=%region_53.54 | all-reduce | flops 12288 | bytes 98304 | tf_op jit(solution)/shard_map/psum | solution.py:250
  807.6 92.1 %reduce-scatter.25.cloned.1.call-done = bf16[96,2880]{1,0:T(8,128)(2,1)} async-done(((bf16[768,2880]{1,0:T(8,128)(2,1)}), bf16[96,2880]{1,0:T(8,128)(2,1)}) %reduce-scatter.25.cloned.1.call-update) | async-done | bytes 552976
  908.4 11.1 %psum.21 = f32[1,2,4608]{2,1,0:T(2,128)S(1)} all-reduce(f32[1,2,4608]{2,1,0:T(2,128)S(1)} %maximum_bitcast_fusion), channel_id=1, replica_groups=mesh['fsdp'=8,'seq'=4] {'seq'}, use_global_device_ids=true, to_apply=%region_39.40 | all-reduce | flops 9216 | bytes 73728 | tf_op jit(solution)/shard_map/psum | solution.py:257
  919.5 31.0 %all_gather.61 = f32[8,2,4608]{2,1,0:T(2,128)S(1)} all-gather(f32[1,2,4608]{2,1,0:T(2,128)S(1)} %psum.21), channel_id=1, replica_groups=mesh['fsdp'=8,'seq'=4] {'fsdp'}, dimensions={0}, use_global_device_ids=true | all-gather | bytes 331776 | tf_op jit(solution)/shard_map/all_gather | solution.py:258
  (423 shorter events, 289.5 us)
Async XLA Ops:
  7.2 113.9 %all-reduce.6.cloned.1.call-start = ((), (), s32[]{:S(2)}) async-start(), calls=%async_computation.31 | async-start | bytes 589824
  44.8 79.0 %copy-start.29 = (bf16[2,96,3072]{2,1,0:T(8,128)(2,1)S(1)}, bf16[2,96,3072]{2,1,0:T(8,128)(2,1)}, u32[]{:S(2)}) copy-start(bf16[2,96,3072]{2,1,0:T(8,128)(2,1)} %param.21) | copy-start | bytes 3538948
  48.8 121.1 %all-gather.13.cloned.1.call-start = ((), (), s32[]{:S(2)}) async-start(), calls=%async_computation.13 | async-start | bytes 1966080 | tf_op jit(solution)/shard_map/all_gather | solution.py:159
  123.7 88.8 %all-gather.15.cloned.1.call-start = ((), (), s32[]{:S(2)}) async-start(), calls=%async_computation.14 | async-start | bytes 3981312 | tf_op jit(solution)/shard_map/all_gather | solution.py:117
  186.8 10.8 %all-to-all-start = ((bf16[4,256,192]{1,2,0:T(8,128)(2,1)}), bf16[4,256,192]{1,2,0:T(8,128)(2,1)S(1)}, u32[]{:S(2)}, u32[]{:S(2)}) async-start(bf16[4,256,192]{1,2,0:T(8,128)(2,1)} %copy.126), calls=%async_computation | async-start | bytes 786432 | tf_op jit(solution)/shard_map/all_to_all | solution.py:163
  190.2 44.7 %all-gather.17.cloned.1.call-start = ((), (), s32[]{:S(2)}) async-start(), calls=%async_computation.15 | async-start | bytes 1966080 | tf_op jit(solution)/shard_map/all_gather | solution.py:168
  216.4 66.4 %reduce-scatter.13.cloned.1.call-start = ((), (), s32[]{:S(2)}) async-start(), calls=%async_computation.16 | async-start | bytes 3932160 | tf_op jit(solution)/shard_map/reduce_scatter | solution.py:172
  244.8 77.9 %all-gather.19.cloned.1.call-start = ((), (), s32[]{:S(2)}) async-start(), calls=%async_computation.17 | async-start | bytes 1966080 | tf_op jit(solution)/shard_map/all_gather | solution.py:159
  285.4 87.2 %all-gather.21.cloned.1.call-start = ((), (), s32[]{:S(2)}) async-start(), calls=%async_computation.18 | async-start | bytes 3981312 | tf_op jit(solution)/shard_map/all_gather | solution.py:117
  340.0 32.6 %all-to-all-start.1 = ((bf16[4,256,192]{1,2,0:T(8,128)(2,1)}), bf16[4,256,192]{1,2,0:T(8,128)(2,1)S(1)}, u32[]{:S(2)}, u32[]{:S(2)}) async-start(bf16[4,256,192]{1,2,0:T(8,128)(2,1)} %copy.131), calls=%async_computation.2 | async-start | bytes 786432 | tf_op jit(solution)/shard_map/all_to_all | solution.py:163
  343.5 51.7 %all-gather.23.cloned.1.call-start = ((), (), s32[]{:S(2)}) async-start(), calls=%async_computation.19 | async-start | bytes 1966080 | tf_op jit(solution)/shard_map/all_gather | solution.py:168
  376.7 40.3 %all-gather.25.cloned.1.call-start = ((), (), s32[]{:S(2)}) async-start(), calls=%async_computation.21 | async-start | bytes 1966080 | tf_op jit(solution)/shard_map/all_gather | solution.py:189
  377.6 88.5 %reduce-scatter.17.cloned.1.call-start = ((), (), s32[]{:S(2)}) async-start(), calls=%async_computation.22 | async-start | bytes 3932160 | tf_op jit(solution)/shard_map/reduce_scatter | solution.py:193
  428.0 78.5 %reduce-scatter.15.cloned.1.call-start = ((), (), s32[]{:S(2)}) async-start(), calls=%async_computation.20 | async-start | bytes 3932160 | tf_op jit(solution)/shard_map/reduce_scatter | solution.py:172
  434.1 157.3 %reduce-scatter.19.cloned.1.call-start = ((), (), s32[]{:S(2)}) async-start(), calls=%async_computation.23 | async-start | bytes 3932160 | tf_op jit(solution)/shard_map/reduce_scatter | solution.py:207
  553.4 61.7 %all-gather.27.cloned.1.call-start = ((), (), s32[]{:S(2)}) async-start(), calls=%async_computation.24 | async-start | bytes 1966080 | tf_op jit(solution)/shard_map/all_gather | solution.py:189
  595.3 68.9 %reduce-scatter.21.cloned.1.call-start = ((), (), s32[]{:S(2)}) async-start(), calls=%async_computation.25 | async-start | bytes 3932160 | tf_op jit(solution)/shard_map/reduce_scatter | solution.py:193
  626.2 135.1 %reduce-scatter.27.cloned.1.call-start = ((), (), s32[]{:S(2)}) async-start(), calls=%async_computation.30 | async-start | bytes 5087232
  643.2 162.8 %reduce-scatter.23.cloned.1.call-start = ((), (), s32[]{:S(2)}) async-start(), calls=%async_computation.26 | async-start | bytes 3932160 | tf_op jit(solution)/shard_map/reduce_scatter | solution.py:207
  710.9 188.8 %reduce-scatter.25.cloned.1.call-start = ((), (), s32[]{:S(2)}) async-start(), calls=%async_computation.29 | async-start | bytes 5087232
  727.4 78.6 %copy-start.48 = (f32[256]{0:T(256)S(1)}, f32[256]{0:T(256)}, u32[]{:S(2)}) copy-start(f32[256]{0:T(256)} %copy-done.47) | copy-start | bytes 3076
  727.4 239.0 %all-reduce.4.cloned.1.call-start = ((), (), s32[]{:S(2)}) async-start(), calls=%async_computation.27 | async-start | bytes 786432 | tf_op jit(solution)/shard_map/psum | solution.py:249
  902.9 65.5 %all-gather.29.cloned.1.call-start = ((), (), s32[]{:S(2)}) async-start(), calls=%async_computation.28 | async-start | bytes 4177920 | tf_op jit(solution)/shard_map/all_gather | solution.py:239
  953.1 11.6 %all-to-all-start.4 = ((f32[8,1,96]{2,1,0:T(1,128)}), f32[8,1,96]{2,1,0:T(1,128)S(1)}, u32[]{:S(2)}, u32[]{:S(2)}) async-start(f32[8,1,96]{2,1,0:T(1,128)} %bitcast.68), calls=%async_computation.10 | async-start | bytes 8192 | tf_op jit(solution)/shard_map/all_to_all | solution.py:285
  (66 other events, 1097.1 us)
Sparse Core Ops, SparseCore 0:
  49.0 72.1 all-reduce.5
  123.8 18.6 all-gather.12
  145.3 67.1 all-gather.14
  216.5 18.3 all-gather.16
  244.9 37.8 reduce-scatter.12
  285.5 19.6 all-gather.18
  307.9 64.5 all-gather.20
  376.8 18.3 all-gather.22
  397.3 19.6 all-gather.24
  428.2 37.8 reduce-scatter.16
  468.6 37.8 reduce-scatter.14
  553.5 37.8 reduce-scatter.18
  595.4 19.6 all-gather.26
  626.3 37.8 reduce-scatter.20
  667.7 93.5 reduce-scatter.26
  764.2 37.6 reduce-scatter.22
  805.4 94.2 reduce-scatter.24
  903.1 32.5 all-reduce.3
  937.8 29.6 all-gather.28
where the time goes:
time: 1020 us; the launch traced here: 1010 us
  waiting for transfers between devices  487 us (48%)
  blocking collectives  203 us (20%)
  matrix products  144 us (14%)
  local copies, waits for them, and re-layouts  90.3 us (9%)
  other arithmetic  55.2 us (5%)
  between operations  15.6 us (2%)
  starting transfers between devices  13.8 us (1%)
    unnamed x22, waiting for transfers between devices  196 us
    reduce_scatter x2, waiting for transfers between devices, per_device(): lax.psum_scatter(feed, 'seq', scatter_dimension=0, tiled=True) + down_b[l]  76.8 us
    all_gather x2, blocking collectives, per_device(): w_qkv.append(lax.all_gather(q_part, 'fsdp', axis=0, tiled=True))  67.3 us
    reduce_scatter x2, waiting for transfers between devices, per_device(): lax.psum_scatter(mm_nt(g_up, w_rest[l][:, :fw]), 'seq', scatter_dimension...  52.9 us
    all_gather x2, waiting for transfers between devices, per_device(): w_rest.append(lax.all_gather(rest, 'fsdp', axis=0, tiled=True))  43.6 us
    psum x1, blocking collectives, per_device(): bias = lax.psum(jnp.stack(bias_grads), ('fsdp', 'seq'))  40.9 us
    reduce_scatter x2, waiting for transfers between devices, per_device(): lax.psum_scatter(mm_nt(g_qkv, w_qkv[l]), 'seq', scatter_dimension=0, tile...  38 us
    all_gather x2, waiting for transfers between devices, per_device(): g_feed_all = lax.all_gather(g_feed, 'seq', axis=0, tiled=True)  36.6 us
  transfers between devices with their start and end apart: 22, of which 16 were waited for; matrix products, arithmetic and copies ran while one was open for 15% of the time, Pallas kernels for 0%

commit v1 on v0

--- a/solution.py
+++ b/solution.py
@@ -200,7 +200,19 @@
         d_gate_a = jnp.sum(g_mid * branch, axis=0)
         grad_out = mm_tn(tok_out, g_branch)
         g_o = mm_nt(g_branch, w_rest[l][:, fw + width :]).astype(BF16)
-        g_o_heads = lax.all_to_all(g_o, "seq", split_axis=1, concat_axis=0, tiled=True)
+        ways, here = (lax.axis_size("seq"), lax.axis_index("seq"))
+        width_2 = g_o.shape[1] // ways
+        shape = list(g_o.shape)
+        shape[1] = width_2
+        height = shape[0]
+        shape[0] = height * ways
+        full = jnp.zeros(shape, g_o.dtype)
+        for mask in range(ways):
+            part_2 = lax.dynamic_slice_in_dim(g_o, (here ^ mask) * width_2, width_2, axis=1)
+            if mask:
+                part_2 = lax.ppermute(part_2, "seq", [(d, d ^ mask) for d in range(ways)])
+            full = lax.dynamic_update_slice_in_dim(full, part_2, (here ^ mask) * height, axis=0)
+        g_o_heads = full
         dq, dk, dv = attend_back(q, k, v, logsum, g_o_heads)
         g_qkv = jnp.concatenate([dq, dk, dv], axis=1)
         grad_qkv = mm_tn(attn_all, g_qkv)

time: 1020 us -> 1020 us (level)
  blocking collectives: 203 us -> 183 us
  waiting for transfers between devices: 487 us -> 503 us
    all_to_all x2 -> x0, blocking collectives: 20.2 us -> none  [per_device(): lax.all_to_all(g_o, 'seq', split_axis=1, concat_axis=0, tiled=True)]
    ppermute x0 -> x6, waiting for transfers between devices: none -> 13.1 us  [per_device(): part_2 = lax.ppermute(part_2, 'seq', [(d, d ^ mask) for d in range(ways)])]
  transfers between devices with their start and end apart: 22 -> 28, of which waited for: 16 -> 18; matrix products, arithmetic and copies ran while one was open for 15% -> 15% of each run, Pallas kernels for 0% -> 0%
where the time goes in v1:
time: 1020 us; the launch traced here: 1010 us
  waiting for transfers between devices  503 us (49%)
  blocking collectives  183 us (18%)
  matrix products  145 us (14%)
  local copies, waits for them, and re-layouts  90.7 us (9%)
  other arithmetic  51.7 us (5%)
  starting transfers between devices  18.9 us (2%)
  between operations  15.7 us (2%)
    unnamed x22, waiting for transfers between devices  200 us
    reduce_scatter x2, waiting for transfers between devices, per_device(): lax.psum_scatter(feed, 'seq', scatter_dimension=0, tiled=True) + down_b[l]  76.8 us
    all_gather x2, blocking collectives, per_device(): w_qkv.append(lax.all_gather(q_part, 'fsdp', axis=0, tiled=True))  67.3 us
    reduce_scatter x2, waiting for transfers between devices, per_device(): lax.psum_scatter(mm_nt(g_up, w_rest[l][:, :fw]), 'seq', scatter_dimension...  52.2 us
    all_gather x2, waiting for transfers between devices, per_device(): w_rest.append(lax.all_gather(rest, 'fsdp', axis=0, tiled=True))  43.6 us
    psum x1, blocking collectives, per_device(): bias = lax.psum(jnp.stack(bias_grads), ('fsdp', 'seq'))  40.9 us
    reduce_scatter x2, waiting for transfers between devices, per_device(): lax.psum_scatter(mm_nt(g_qkv, w_qkv[l]), 'seq', scatter_dimension=0, tile...  38 us
    all_gather x2, waiting for transfers between devices, per_device(): g_feed_all = lax.all_gather(g_feed, 'seq', axis=0, tiled=True)  36.6 us
  transfers between devices with their start and end apart: 28, of which 18 were waited for; matrix products, arithmetic and copies ran while one was open for 15% of the time, Pallas kernels for 0%

profile of v1, /device:TPU:0, one launch (start us, length us, event | category | flops | bytes accessed | tf_op | source)
XLA Modules:
  0.0 1007.7 jit_solution(6210588304399299064)
XLA Ops:
  12.4 32.4 %all-gather.2 = bf16[8,1,3456]{2,1,0:T(2,128)(2,1)S(1)} all-gather(bf16[1,1,3456]{2,1,0:T(2,128)(2,1)S(1)} %reshape.383), channel_id=2, replica_groups=mesh['fsdp'=8,'seq'=4] {'fsdp'}, dimensions={0}, use_global_device_ids=true | all-gather | bytes 62208 | tf_op jit(solution)/shard_map/all_gather | solution.py:131
  50.2 71.0 %all-reduce.6.cloned.1.call-done = f32[8,2,4608]{2,1,0:T(2,128)} async-done(((f32[8,2,4608]{2,1,0:T(2,128)}), f32[8,2,4608]{2,1,0:T(2,128)}) %all-reduce.6.cloned.1.call-update) | async-done | bytes 294928
  135.6 34.4 %all_gather.51 = bf16[768,576]{1,0:T(8,128)(2,1)S(1)} all-gather(bf16[96,576]{1,0:T(8,128)(2,1)S(1)} %copy.121), channel_id=1, replica_groups=mesh['fsdp'=8,'seq'=4] {'fsdp'}, dimensions={0}, use_global_device_ids=true | all-gather | bytes 995328 | tf_op jit(solution)/shard_map/all_gather | solution.py:115
  173.0 6.9 fusion.3
  197.6 14.9 %all-gather.15.cloned.1.call-done = bf16[768,2304]{1,0:T(8,128)(2,1)} async-done(((bf16[96,2304]{1,0:T(8,128)(2,1)}), bf16[768,2304]{1,0:T(8,128)(2,1)}) %all-gather.15.cloned.1.call-update) | async-done | bytes 3538960 | tf_op jit(solution)/shard_map/all_gather | solution.py:117
  216.7 18.2 %all-gather.17.cloned.1.call-done = bf16[1024,768]{1,0:T(8,128)(2,1)} async-done(((bf16[256,768]{1,0:T(8,128)(2,1)}), bf16[1024,768]{1,0:T(8,128)(2,1)}) %all-gather.17.cloned.1.call-update) | async-done | bytes 1572880 | tf_op jit(solution)/shard_map/all_gather | solution.py:168
  244.9 37.9 %reduce-scatter.13.cloned.1.call-done = f32[256,768]{1,0:T(8,128)} async-done(((f32[1024,768]{1,0:T(8,128)}), f32[256,768]{1,0:T(8,128)}) %reduce-scatter.13.cloned.1.call-update) | async-done | bytes 786448 | tf_op jit(solution)/shard_map/reduce_scatter | solution.py:172
  289.8 32.9 %all_gather.55 = bf16[768,576]{1,0:T(8,128)(2,1)S(1)} all-gather(bf16[96,576]{1,0:T(8,128)(2,1)S(1)} %copy.127), channel_id=1, replica_groups=mesh['fsdp'=8,'seq'=4] {'fsdp'}, dimensions={0}, use_global_device_ids=true | all-gather | bytes 995328 | tf_op jit(solution)/shard_map/all_gather | solution.py:115
  326.3 6.9 fusion.2
  343.8 28.8 %all-gather.21.cloned.1.call-done = bf16[768,2304]{1,0:T(8,128)(2,1)} async-done(((bf16[96,2304]{1,0:T(8,128)(2,1)}), bf16[768,2304]{1,0:T(8,128)(2,1)}) %all-gather.21.cloned.1.call-update) | async-done | bytes 3538960 | tf_op jit(solution)/shard_map/all_gather | solution.py:117
  377.7 17.5 %all-gather.23.cloned.1.call-done = bf16[1024,768]{1,0:T(8,128)(2,1)} async-done(((bf16[256,768]{1,0:T(8,128)(2,1)}), bf16[1024,768]{1,0:T(8,128)(2,1)}) %all-gather.23.cloned.1.call-update) | async-done | bytes 1572880 | tf_op jit(solution)/shard_map/all_gather | solution.py:168
  400.0 17.0 %all-gather.25.cloned.1.call-done = bf16[1024,768]{1,0:T(8,128)(2,1)} async-done(((bf16[256,768]{1,0:T(8,128)(2,1)}), bf16[1024,768]{1,0:T(8,128)(2,1)}) %all-gather.25.cloned.1.call-update) | async-done | bytes 1572880 | tf_op jit(solution)/shard_map/all_gather | solution.py:189
  434.7 31.4 %reduce-scatter.17.cloned.1.call-done = f32[256,768]{1,0:T(8,128)} async-done(((f32[1024,768]{1,0:T(8,128)}), f32[256,768]{1,0:T(8,128)}) %reduce-scatter.17.cloned.1.call-update) | async-done | bytes 786448 | tf_op jit(solution)/shard_map/reduce_scatter | solution.py:193
  467.6 38.9 %reduce-scatter.15.cloned.1.call-done = f32[256,768]{1,0:T(8,128)} async-done(((f32[1024,768]{1,0:T(8,128)}), f32[256,768]{1,0:T(8,128)}) %reduce-scatter.15.cloned.1.call-update) | async-done | bytes 786448 | tf_op jit(solution)/shard_map/reduce_scatter | solution.py:172
  522.2 7.5 convert_reduce_fusion.5
  552.5 38.0 %reduce-scatter.19.cloned.1.call-done = f32[256,768]{1,0:T(8,128)} async-done(((f32[1024,768]{1,0:T(8,128)}), f32[256,768]{1,0:T(8,128)}) %reduce-scatter.19.cloned.1.call-update) | async-done | bytes 786448 | tf_op jit(solution)/shard_map/reduce_scatter | solution.py:219
  594.6 19.6 %all-gather.27.cloned.1.call-done = bf16[1024,768]{1,0:T(8,128)(2,1)} async-done(((bf16[256,768]{1,0:T(8,128)(2,1)}), bf16[1024,768]{1,0:T(8,128)(2,1)}) %all-gather.27.cloned.1.call-update) | async-done | bytes 1572880 | tf_op jit(solution)/shard_map/all_gather | solution.py:189
  642.5 20.8 %reduce-scatter.21.cloned.1.call-done = f32[256,768]{1,0:T(8,128)} async-done(((f32[1024,768]{1,0:T(8,128)}), f32[256,768]{1,0:T(8,128)}) %reduce-scatter.21.cloned.1.call-update) | async-done | bytes 786448 | tf_op jit(solution)/shard_map/reduce_scatter | solution.py:193
  678.4 11.7 %multiply_reduce_fusion = (f32[3,1024]{1,0:T(4,128)S(1)}, f32[3,1024,1024]{1,2,0:T(8,128)}) fusion(f32[3,1024,1024]{1,2,0:T(8,128)} %fusion.3, bf16[3,1024,64]{1,2,0:T(8,128)(2,1)S(1)} %bitcast.259, bf16[3,1024,64]{1,2,0:T(8,128)(2,1)S(1)} %bitcast.256), kind=kOutput, calls=%fused_computation.7 | convolution fusion | flops 408941568 | bytes 25964544 | tf_op jit(solution)/shard_map/hqd,hkd->hqk/dot_general | solution.py:62
  723.4 36.9 %reduce-scatter.27.cloned.1.call-done = bf16[96,2880]{1,0:T(8,128)(2,1)} async-done(((bf16[768,2880]{1,0:T(8,128)(2,1)}), bf16[96,2880]{1,0:T(8,128)(2,1)}) %reduce-scatter.27.cloned.1.call-update) | async-done | bytes 552976
  762.2 40.9 %psum.22 = f32[2,8,768]{2,0,1:T(2,128)S(1)} all-reduce(f32[2,8,768]{2,0,1:T(2,128)S(1)} %pad_maximum_fusion.14), channel_id=1, replica_groups=mesh['fsdp'=8,'seq'=4] {'fsdp','seq'}, use_global_device_ids=true, to_apply=%region_53.54 | all-reduce | flops 12288 | bytes 98304 | tf_op jit(solution)/shard_map/psum | solution.py:262
  806.7 92.1 %reduce-scatter.25.cloned.1.call-done = bf16[96,2880]{1,0:T(8,128)(2,1)} async-done(((bf16[768,2880]{1,0:T(8,128)(2,1)}), bf16[96,2880]{1,0:T(8,128)(2,1)}) %reduce-scatter.25.cloned.1.call-update) | async-done | bytes 552976
  907.5 11.0 %psum.21 = f32[1,2,4608]{2,1,0:T(2,128)S(1)} all-reduce(f32[1,2,4608]{2,1,0:T(2,128)S(1)} %maximum_bitcast_fusion), channel_id=1, replica_groups=mesh['fsdp'=8,'seq'=4] {'seq'}, use_global_device_ids=true, to_apply=%region_39.40 | all-reduce | flops 9216 | bytes 73728 | tf_op jit(solution)/shard_map/psum | solution.py:269
  918.6 31.0 %all_gather.61 = f32[8,2,4608]{2,1,0:T(2,128)S(1)} all-gather(f32[1,2,4608]{2,1,0:T(2,128)S(1)} %psum.21), channel_id=1, replica_groups=mesh['fsdp'=8,'seq'=4] {'fsdp'}, dimensions={0}, use_global_device_ids=true | all-gather | bytes 331776 | tf_op jit(solution)/shard_map/all_gather | solution.py:270
  (440 shorter events, 293.4 us)
Async XLA Ops:
  7.2 113.9 %all-reduce.6.cloned.1.call-start = ((), (), s32[]{:S(2)}) async-start(), calls=%async_computation.29 | async-start | bytes 589824
  48.8 121.1 %all-gather.13.cloned.1.call-start = ((), (), s32[]{:S(2)}) async-start(), calls=%async_computation.11 | async-start | bytes 1966080 | tf_op jit(solution)/shard_map/all_gather | solution.py:159
  123.7 88.8 %all-gather.15.cloned.1.call-start = ((), (), s32[]{:S(2)}) async-start(), calls=%async_computation.12 | async-start | bytes 3981312 | tf_op jit(solution)/shard_map/all_gather | solution.py:117
  186.8 10.8 %all-to-all-start = ((bf16[4,256,192]{1,2,0:T(8,128)(2,1)}), bf16[4,256,192]{1,2,0:T(8,128)(2,1)S(1)}, u32[]{:S(2)}, u32[]{:S(2)}) async-start(bf16[4,256,192]{1,2,0:T(8,128)(2,1)} %copy.124), calls=%async_computation | async-start | bytes 786432 | tf_op jit(solution)/shard_map/all_to_all | solution.py:163
  190.2 44.7 %all-gather.17.cloned.1.call-start = ((), (), s32[]{:S(2)}) async-start(), calls=%async_computation.13 | async-start | bytes 1966080 | tf_op jit(solution)/shard_map/all_gather | solution.py:168
  216.4 66.4 %reduce-scatter.13.cloned.1.call-start = ((), (), s32[]{:S(2)}) async-start(), calls=%async_computation.14 | async-start | bytes 3932160 | tf_op jit(solution)/shard_map/reduce_scatter | solution.py:172
  244.8 77.9 %all-gather.19.cloned.1.call-start = ((), (), s32[]{:S(2)}) async-start(), calls=%async_computation.15 | async-start | bytes 1966080 | tf_op jit(solution)/shard_map/all_gather | solution.py:159
  285.4 87.2 %all-gather.21.cloned.1.call-start = ((), (), s32[]{:S(2)}) async-start(), calls=%async_computation.16 | async-start | bytes 3981312 | tf_op jit(solution)/shard_map/all_gather | solution.py:117
  340.0 32.6 %all-to-all-start.1 = ((bf16[4,256,192]{1,2,0:T(8,128)(2,1)}), bf16[4,256,192]{1,2,0:T(8,128)(2,1)S(1)}, u32[]{:S(2)}, u32[]{:S(2)}) async-start(bf16[4,256,192]{1,2,0:T(8,128)(2,1)} %copy.129), calls=%async_computation.2 | async-start | bytes 786432 | tf_op jit(solution)/shard_map/all_to_all | solution.py:163
  343.5 51.7 %all-gather.23.cloned.1.call-start = ((), (), s32[]{:S(2)}) async-start(), calls=%async_computation.17 | async-start | bytes 1966080 | tf_op jit(solution)/shard_map/all_gather | solution.py:168
  376.7 40.3 %all-gather.25.cloned.1.call-start = ((), (), s32[]{:S(2)}) async-start(), calls=%async_computation.19 | async-start | bytes 1966080 | tf_op jit(solution)/shard_map/all_gather | solution.py:189
  377.6 88.5 %reduce-scatter.17.cloned.1.call-start = ((), (), s32[]{:S(2)}) async-start(), calls=%async_computation.20 | async-start | bytes 3932160 | tf_op jit(solution)/shard_map/reduce_scatter | solution.py:193
  428.0 78.5 %reduce-scatter.15.cloned.1.call-start = ((), (), s32[]{:S(2)}) async-start(), calls=%async_computation.18 | async-start | bytes 3932160 | tf_op jit(solution)/shard_map/reduce_scatter | solution.py:172
  434.1 156.4 %reduce-scatter.19.cloned.1.call-start = ((), (), s32[]{:S(2)}) async-start(), calls=%async_computation.21 | async-start | bytes 3932160 | tf_op jit(solution)/shard_map/reduce_scatter | solution.py:219
  512.4 8.9 collective-permute-start.2
  552.4 61.7 %all-gather.27.cloned.1.call-start = ((), (), s32[]{:S(2)}) async-start(), calls=%async_computation.22 | async-start | bytes 1966080 | tf_op jit(solution)/shard_map/all_gather | solution.py:189
  594.4 68.9 %reduce-scatter.21.cloned.1.call-start = ((), (), s32[]{:S(2)}) async-start(), calls=%async_computation.23 | async-start | bytes 3932160 | tf_op jit(solution)/shard_map/reduce_scatter | solution.py:193
  625.2 135.1 %reduce-scatter.27.cloned.1.call-start = ((), (), s32[]{:S(2)}) async-start(), calls=%async_computation.28 | async-start | bytes 5087232
  642.2 162.8 %reduce-scatter.23.cloned.1.call-start = ((), (), s32[]{:S(2)}) async-start(), calls=%async_computation.24 | async-start | bytes 3932160 | tf_op jit(solution)/shard_map/reduce_scatter | solution.py:219
  669.5 8.7 collective-permute-start.5
  705.7 193.0 %reduce-scatter.25.cloned.1.call-start = ((), (), s32[]{:S(2)}) async-start(), calls=%async_computation.27 | async-start | bytes 5087232
  722.2 243.3 %all-reduce.4.cloned.1.call-start = ((), (), s32[]{:S(2)}) async-start(), calls=%async_computation.25 | async-start | bytes 786432 | tf_op jit(solution)/shard_map/psum | solution.py:261
  902.0 65.5 %all-gather.29.cloned.1.call-start = ((), (), s32[]{:S(2)}) async-start(), calls=%async_computation.26 | async-start | bytes 4177920 | tf_op jit(solution)/shard_map/all_gather | solution.py:251
  952.1 11.6 %all-to-all-start.2 = ((f32[8,1,96]{2,1,0:T(1,128)}), f32[8,1,96]{2,1,0:T(1,128)S(1)}, u32[]{:S(2)}, u32[]{:S(2)}) async-start(f32[8,1,96]{2,1,0:T(1,128)} %bitcast.68), calls=%async_computation.8 | async-start | bytes 8192 | tf_op jit(solution)/shard_map/all_to_all | solution.py:297
  (72 other events, 1248.2 us)
Sparse Core Ops, SparseCore 0:
  49.0 72.1 all-reduce.5
  123.8 18.6 all-gather.12
  145.3 67.1 all-gather.14
  216.5 18.3 all-gather.16
  244.9 37.8 reduce-scatter.12
  285.5 19.6 all-gather.18
  307.9 64.5 all-gather.20
  376.8 18.3 all-gather.22
  397.3 19.6 all-gather.24
  428.2 37.8 reduce-scatter.16
  468.6 37.8 reduce-scatter.14
  552.6 37.8 reduce-scatter.18
  594.5 19.6 all-gather.26
  625.3 37.8 reduce-scatter.20
  666.7 93.5 reduce-scatter.26
  763.3 37.6 reduce-scatter.22
  804.5 94.2 reduce-scatter.24
  902.1 32.6 all-reduce.3
  936.9 29.6 all-gather.28
